TPU v7x, 32 devices: a whole 2x2x4 slice. The times are simulated.
32 devices in a mesh: fsdp: 16 (over z, y, core), grp: 2 (over x).
Axes of the slice: x: 2, y: 2, z: 4, core: 2. Of those that a mesh axis runs over, the one named last changes fastest.
Arguments:
- hidden: bfloat16 [8192, 3072], P('fsdp', 'grp'), may hold values from -16 to 16
- queries: bfloat16 [8192, 1536], P('fsdp', 'grp'), may hold values from -6 to 6
- attn_keys: bfloat16 [8192, 1536], P('fsdp', 'grp'), may hold values from -6 to 6
- w_value: bfloat16 [1536, 3072], P('fsdp', 'grp'), may hold values from -1 to 1
- w_out: bfloat16 [1536, 3072], P('fsdp', 'grp'), may hold values from -1 to 1
- alpha: float32 [3072], P('grp'), may hold values from 0.05 to 0.5
- out_grad: bfloat16 [8192, 3072], P('fsdp', 'grp'), may hold values from -6 to 6
Outputs:
- new_hidden: bfloat16 [8192, 3072], P('fsdp', 'grp')
- grad_hidden: bfloat16 [8192, 3072], P('fsdp', 'grp')
- grad_queries: bfloat16 [8192, 1536], P('fsdp', 'grp')
- grad_keys: bfloat16 [8192, 1536], P('fsdp', 'grp')
- grad_w_value: float32 [1536, 3072], P('fsdp', 'grp')
- grad_w_out: float32 [1536, 3072], P('fsdp', 'grp')
All inputs are finite; a program needn't handle non-finite values.
Results may differ from a plain program's by a relative error of at most 0.012.
The roundings to bfloat16 on the way count: a program that leaves them out, or rounds other values in their place, can miss the bound.
Values may be sent and summed in bfloat16 or wider, within the bound.
A program may use at most 192 MiB of HBM per device.

v0:
```python
import jax
import jax.numpy as jnp
from jax import lax
from jax.sharding import PartitionSpec as P

D = 3072
HS = 128
EPS = 1e-06


def contract_last(left, right):
    return lax.dot_general(
        left, right, (((1,), (1,)), ((), ())), preferred_element_type=jnp.float32
    )


def contract_first(left, right):
    return lax.dot_general(
        left, right, (((0,), (0,)), ((), ())), preferred_element_type=jnp.float32
    )


def causal_probs(query_head, key_head):
    length = query_head.shape[0]
    score_scale = query_head.shape[1] ** (-0.5)
    scores = contract_last(query_head, key_head) * score_scale
    row_pos = lax.broadcasted_iota(jnp.int32, (length, length), 0)
    col_pos = lax.broadcasted_iota(jnp.int32, (length, length), 1)
    scores = jnp.where(row_pos >= col_pos, scores, -1e30)
    row_peak = jnp.max(scores, axis=1, keepdims=True)
    exp_terms = jnp.exp(scores - row_peak)
    return exp_terms / jnp.sum(exp_terms, axis=1, keepdims=True)


def head_forward(items):
    query_head, key_head, value_head = items
    attn_prob = causal_probs(query_head, key_head)
    return jnp.dot(
        attn_prob.astype(jnp.bfloat16), value_head, preferred_element_type=jnp.float32
    ).astype(jnp.bfloat16)


def head_backward(items):
    query_head, key_head, value_head, grad_head = items
    score_scale = query_head.shape[1] ** (-0.5)
    attn_prob = causal_probs(query_head, key_head)
    prob_half = attn_prob.astype(jnp.bfloat16)
    grad_prob = contract_last(grad_head, value_head)
    row_delta = jnp.sum(attn_prob * grad_prob, axis=1, keepdims=True)
    grad_score = (attn_prob * (grad_prob - row_delta)).astype(jnp.bfloat16)
    grad_query = (
        jnp.dot(grad_score, key_head, preferred_element_type=jnp.float32) * score_scale
    ).astype(jnp.bfloat16)
    grad_key = (contract_first(grad_score, query_head) * score_scale).astype(jnp.bfloat16)
    grad_value = contract_first(prob_half, grad_head).astype(jnp.bfloat16)
    return (grad_query, grad_key, grad_value)


def split_heads(block):
    return block.reshape(block.shape[0], -1, HS).transpose(1, 0, 2)


def join_heads(stacked):
    return stacked.transpose(1, 0, 2).reshape(stacked.shape[1], -1)


def shards(hidden, queries, attn_keys, w_value, w_out, alpha, out_grad):
    half_width = hidden.shape[1]
    value_rows = w_value.astype(jnp.float32)
    out_rows = w_out.astype(jnp.float32)
    row_sums = lax.psum(
        (jnp.sum(value_rows * value_rows, axis=1), jnp.sum(out_rows * out_rows, axis=1)), "grp"
    )
    norm_v = jnp.sqrt(row_sums[0] + EPS)[:, None]
    norm_o = jnp.sqrt(row_sums[1] + EPS)[:, None]
    unit_v = value_rows / norm_v
    unit_o = out_rows / norm_o
    weight_v, weight_o = (
        lax.all_gather(unit_v.astype(jnp.bfloat16), "fsdp", axis=0, tiled=True),
        lax.all_gather(unit_o.astype(jnp.bfloat16), "fsdp", axis=0, tiled=True),
    )
    value_parts = contract_last(hidden, weight_v)
    values_mine = lax.psum_scatter(value_parts, "grp", scatter_dimension=1, tiled=True).astype(
        jnp.bfloat16
    )
    q_heads = split_heads(queries)
    k_heads = split_heads(attn_keys)
    v_heads = split_heads(values_mine)
    attn_mine = join_heads(lax.map(head_forward, (q_heads, k_heads, v_heads)))
    attn_all = lax.all_gather(attn_mine, "grp", axis=1, tiled=True)
    proj = jnp.dot(attn_all, weight_o, preferred_element_type=jnp.float32)
    hidden_f = hidden.astype(jnp.float32)
    keep_rate = 1.0 - alpha
    moments = lax.psum(
        (
            jnp.sum(proj * proj, axis=1),
            jnp.sum(keep_rate * keep_rate * hidden_f * hidden_f, axis=1),
            jnp.sum(keep_rate * alpha * hidden_f * proj, axis=1),
            jnp.sum(alpha * alpha * proj * proj, axis=1),
        ),
        "grp",
    )
    proj_rs = lax.rsqrt(moments[0] / D + EPS)[:, None]
    cross_sum = moments[2][:, None]
    alpha_sum = moments[3][:, None]
    mix_mean = (moments[1][:, None] + 2.0 * proj_rs * cross_sum + proj_rs * proj_rs * alpha_sum) / D
    mix_rs = lax.rsqrt(mix_mean + EPS)
    mixed = hidden_f + alpha * (proj * proj_rs - hidden_f)
    new_hidden = (mixed * mix_rs).astype(jnp.bfloat16)
    grad_out = out_grad.astype(jnp.float32)
    grad_sums = lax.psum(
        (
            jnp.sum(grad_out * keep_rate * hidden_f, axis=1),
            jnp.sum(grad_out * alpha * proj, axis=1),
        ),
        "grp",
    )
    grad_mean = (grad_sums[0][:, None] + proj_rs * grad_sums[1][:, None]) / D
    grad_mix = mix_rs * (grad_out - mixed * mix_rs * mix_rs * grad_mean)
    grad_pn = grad_mix * alpha
    proj_mean = (
        mix_rs * grad_sums[1][:, None]
        - mix_rs * mix_rs * mix_rs * grad_mean * (cross_sum + proj_rs * alpha_sum)
    ) / D
    grad_res = grad_mix * keep_rate
    grad_proj = proj_rs * (grad_pn - proj * proj_rs * proj_rs * proj_mean)
    grad_proj_b = grad_proj.astype(jnp.bfloat16)
    grad_attn_parts = contract_last(grad_proj_b, weight_o)
    grad_attn = lax.psum_scatter(grad_attn_parts, "grp", scatter_dimension=1, tiled=True).astype(
        jnp.bfloat16
    )
    grad_q, grad_k, grad_v = lax.map(
        head_backward, (q_heads, k_heads, v_heads, split_heads(grad_attn))
    )
    grad_values = lax.all_gather(join_heads(grad_v), "grp", axis=1, tiled=True)
    grad_hidden = (
        grad_res + jnp.dot(grad_values, weight_v, preferred_element_type=jnp.float32)
    ).astype(jnp.bfloat16)
    owned = lax.psum_scatter(
        jnp.concatenate(
            (contract_first(grad_values, hidden), contract_first(attn_all, grad_proj_b)), axis=1
        ),
        "fsdp",
        scatter_dimension=0,
        tiled=True,
    )
    gw_v_own = owned[:, :half_width]
    gw_o_own = owned[:, half_width:]
    row_dot = lax.psum(
        (jnp.sum(gw_v_own * unit_v, axis=1), jnp.sum(gw_o_own * unit_o, axis=1)), "grp"
    )
    grad_w_value = (gw_v_own - unit_v * row_dot[0][:, None]) / norm_v
    grad_w_out = (gw_o_own - unit_o * row_dot[1][:, None]) / norm_o
    return (
        new_hidden,
        grad_hidden,
        join_heads(grad_q),
        join_heads(grad_k),
        grad_w_value,
        grad_w_out,
    )


def solution(mesh):
    placed = (
        P("fsdp", "grp"),
        P("fsdp", "grp"),
        P("fsdp", "grp"),
        P("fsdp", "grp"),
        P("fsdp", "grp"),
        P("grp"),
        P("fsdp", "grp"),
    )
    return jax.shard_map(
        shards,
        mesh=mesh,
        in_specs=placed,
        out_specs=(
            P("fsdp", "grp"),
            P("fsdp", "grp"),
            P("fsdp", "grp"),
            P("fsdp", "grp"),
            P("fsdp", "grp"),
            P("fsdp", "grp"),
        ),
        check_vma=False,
    )
```

profile of v0, /device:TPU:0, one launch (start us, length us, event | category | flops | bytes accessed | tf_op | source)
XLA Modules:
  0.0 593.8 jit_solution(14473532207321060292)
XLA Ops:
  8.5 5.9 all-reduce.2
  14.4 1.8 fusion.60
  16.2 55.0 %all-gather.5.cloned.1.call-done = bf16[1536,1536]{1,0:T(8,128)(2,1)} async-done(((bf16[96,1536]{1,0:T(8,128)(2,1)}), bf16[1536,1536]{1,0:T(8,128)(2,1)}) %all-gather.5.cloned.1.call-update) | async-done | bytes 4718608 | tf_op jit(solution)/shard_map/all_gather | solution.py:79
  71.3 7.1 %convolution_bitcast_fusion = f32[512,1536]{0,1:T(8,128)} fusion(bf16[1536,1536]{1,0:T(8,128)(2,1)} %all-gather.5.cloned.1.call-done, bf16[512,1536]{1,0:T(8,128)(2,1)} %param.11), kind=kOutput, calls=%fused_computation.68 | convolution fusion | flops 2415919104 | bytes 9437184 | tf_op jit(solution)/shard_map/dot_general | solution.py:12
  81.6 39.0 %reduce-scatter.6.cloned.1.call-done = f32[512,768]{0,1:T(8,128)} async-done(((f32[512,1536]{0,1:T(8,128)}), f32[512,768]{0,1:T(8,128)}) %reduce-scatter.6.cloned.1.call-update) | async-done | bytes 1572880 | tf_op jit(solution)/shard_map/reduce_scatter | solution.py:83
  123.3 11.8 %while.24 = (s32[]{:T(128)}, bf16[6,512,128]{1,2,0:T(8,128)(2,1)S(1)}, bf16[6,512,128]{2,1,0:T(8,128)(2,1)S(1)}, bf16[6,512,128]{2,1,0:T(8,128)(2,1)S(1)}, bf16[6,512,128]{2,1,0:T(8,128)(2,1)}, /*index=5*/s32[]{:T(128)}) while((s32[]{:T(128)}, bf16[6,512,128]{1,2,0:T(8,128)(2,1)S(1)}, bf16[6,512,128]{2,1,0:T(8,128)(2,1)S(1)}, ...), condition=%wide.region_6.7_spmd, body=%wide.region_3.6_spmd.sunk | while | flops 136641536 | bytes 4205653 | solution.py:89
  136.1 40.5 %all-gather.9.cloned.1.call-done = bf16[1536,1536]{1,0:T(8,128)(2,1)} async-done(((bf16[96,1536]{1,0:T(8,128)(2,1)}), bf16[1536,1536]{1,0:T(8,128)(2,1)}) %all-gather.9.cloned.1.call-update) | async-done | bytes 4718608 | tf_op jit(solution)/shard_map/all_gather | solution.py:80
  176.6 27.7 %all-gather.7.cloned.1.call-done = bf16[512,1536]{0,1:T(8,128)(2,1)} async-done(((bf16[512,768]{0,1:T(8,128)(2,1)}), bf16[512,1536]{0,1:T(8,128)(2,1)}) %all-gather.7.cloned.1.call-update) | async-done | bytes 1572880 | tf_op jit(solution)/shard_map/all_gather | solution.py:90
  204.3 8.4 %fusion.43 = (f32[512]{0:T(512)S(1)}, f32[512]{0:T(512)S(1)}, f32[512]{0:T(512)S(1)}, f32[512]{0:T(512)S(1)}, f32[512]{0:T(512)S(1)}, /*index=5*/f32[512]{0:T(512)S(1)}, f32[512,1536]{1,0:T(8,128)S(1)}) fusion(bf16[512,1536]{1,0:T(8,128)(2,1)} %param.17, f32[1536]{0:T(1024)S(1)} %copy-done.14, f32[1536]{0:T(1024)S(1)} %get-tuple-element.182, ...), kind=kOutput, calls=%fused_computation.72 | convolution fusion | flops 2430858240 | bytes 12625920 | tf_op jit(solution)/shard_map/dot_general | solution.py:91
  212.7 6.9 %all-reduce.1 = (f32[512]{0:T(512)S(1)}, f32[512]{0:T(512)S(1)}, f32[512]{0:T(512)S(1)}, f32[512]{0:T(512)S(1)}, f32[512]{0:T(512)S(1)}, /*index=5*/f32[512]{0:T(512)S(1)}) all-reduce(f32[512]{0:T(512)S(1)} %get-tuple-element.126, f32[512]{0:T(512)S(1)} %get-tuple-element.130, ...), channel_id=1, replica_groups=mesh['fsdp'=16,'grp'=2] {'grp'}, use_global_device_ids=true, to_apply=%region_16.17 | all-reduce | flops 3072 | bytes 24576 | tf_op jit(solution)/shard_map/psum | solution.py:94
  219.7 4.5 multiply_convert_fusion.1
  225.4 4.3 fusion.65
  229.7 44.7 %reduce-scatter.8.cloned.1.call-done = f32[512,768]{1,0:T(8,128)} async-done(((f32[512,1536]{1,0:T(8,128)}), f32[512,768]{1,0:T(8,128)}) %reduce-scatter.8.cloned.1.call-update) | async-done | bytes 1572880 | tf_op jit(solution)/shard_map/reduce_scatter | solution.py:129
  278.2 47.0 %while.25 = (s32[]{:T(128)}, bf16[6,512,128]{1,2,0:T(8,128)(2,1)}, bf16[6,512,128]{1,2,0:T(8,128)(2,1)S(1)}, bf16[6,512,128]{1,2,0:T(8,128)(2,1)S(1)}, bf16[6,51...) while((s32[]{:T(128)}, bf16[6,512,128]{1,2,0:T(8,128)(2,1)}, ...), condition=%wide.region_26.27_spmd, body=%wide.region_22.26_spmd.sunk | while | flops 340589056 | bytes 11821177 | solution.py:132
  326.2 8.5 %fusion.67 = f32[1536,1536]{0,1:T(8,128)} fusion(bf16[512,1536]{0,1:T(8,128)(2,1)} %all-gather.7.cloned.1.call-done, bf16[512,1536]{1,0:T(8,128)(2,1)} %copy-done.11), kind=kOutput, calls=%fused_computation.114 | convolution fusion | flops 2415919104 | bytes 12582912 | tf_op jit(solution)/shard_map/dot_general | solution.py:18
  334.7 18.8 %all-gather.11.cloned.1.call-done = bf16[512,1536]{0,1:T(8,128)(2,1)} async-done(((bf16[512,768]{0,1:T(8,128)(2,1)}), bf16[512,1536]{0,1:T(8,128)(2,1)}) %all-gather.11.cloned.1.call-update) | async-done | bytes 1572880 | tf_op jit(solution)/shard_map/all_gather | solution.py:135
  353.5 4.2 fusion.66
  357.8 7.2 %pad_maximum_fusion = f32[1536,3072]{0,1:T(8,128)} fusion(f32[1536,1536]{0,1:T(8,128)S(1)} %copy-done, f32[1536,1536]{0,1:T(8,128)S(1)} %fusion.66), kind=kLoop, calls=%fused_computation.57 | loop fusion | flops 4718592 | bytes 37748736 | tf_op jit(solution)/shard_map/concatenate | solution.py:140
  365.0 18.7 %copy.57 = f32[1536,3072]{1,0:T(8,128)} copy(f32[1536,3072]{0,1:T(8,128)} %pad_maximum_fusion) | data formatting | bytes 37748736
  387.1 9.9 %fusion.51 = bf16[512,1536]{1,0:T(8,128)(2,1)} fusion(bf16[512,1536]{0,1:T(8,128)(2,1)} %all-gather.11.cloned.1.call-done, bf16[1536,1536]{1,0:T(8,128)(2,1)} %all-gather.5.cloned.1.call-done, bf16[512,1536]{1,0:T(8,128)(2,1)S(1)} %copy-done.9, f32[512]{0:T(512)S(1)} %get-tuple-element.187, f32[1536]{0:T(1024)S(1)} %get-tuple-element.185, ...), kind=kOutput, calls=%fused_computation.82 | convolution fusion | flops 2426929152 | bytes 14174208 | tf_op jit(solution)/shard_map/dot_general | solution.py:137
  397.0 180.8 %reduce-scatter.10.cloned.1.call-done = f32[96,3072]{1,0:T(8,128)} async-done(((f32[1536,3072]{1,0:T(8,128)}), f32[96,3072]{1,0:T(8,128)}) %reduce-scatter.10.cloned.1.call-update) | async-done | bytes 1179664 | tf_op jit(solution)/shard_map/reduce_scatter | solution.py:139
  577.9 1.6 multiply_reduce_fusion.2
  579.5 4.9 all-reduce
  584.4 2.5 subtract_divide_fusion
  (168 shorter events, 75.7 us)
Async XLA Ops:
  7.2 64.1 %all-gather.5.cloned.1.call-start = ((), (), s32[]{:S(2)}) async-start(), calls=%async_computation.3 | async-start | bytes 5013504 | tf_op jit(solution)/shard_map/all_gather | solution.py:79
  16.2 104.4 %reduce-scatter.6.cloned.1.call-start = ((), (), s32[]{:S(2)}) async-start(), calls=%async_computation.4 | async-start | bytes 4718592 | tf_op jit(solution)/shard_map/reduce_scatter | solution.py:83
  78.4 1.0 copy-start.2
  78.4 1.9 copy-start.12
  78.4 2.5 copy-start.13
  78.4 98.1 %all-gather.9.cloned.1.call-start = ((), (), s32[]{:S(2)}) async-start(), calls=%async_computation.6 | async-start | bytes 5013504 | tf_op jit(solution)/shard_map/all_gather | solution.py:80
  80.2 124.1 %all-gather.7.cloned.1.call-start = ((), (), s32[]{:S(2)}) async-start(), calls=%async_computation.5 | async-start | bytes 2359296 | tf_op jit(solution)/shard_map/all_gather | solution.py:90
  123.3 12.8 %copy-start.14 = (f32[1536]{0:T(1024)S(1)}, f32[1536]{0:T(1024)}, u32[]{:S(2)}) copy-start(f32[1536]{0:T(1024)} %param.16) | copy-start | bytes 18436
  135.1 0.9 copy-start.5
  135.1 69.2 %copy-start.7 = (bf16[6,512,128]{2,1,0:T(8,128)(2,1)}, bf16[6,512,128]{2,1,0:T(8,128)(2,1)S(1)}, u32[]{:S(2)}) copy-start(bf16[6,512,128]{2,1,0:T(8,128)(2,1)S(1)} %get-tuple-element.351) | copy-start | bytes 2359300
  135.1 69.2 %copy-start.8 = (bf16[6,512,128]{2,1,0:T(8,128)(2,1)}, bf16[6,512,128]{2,1,0:T(8,128)(2,1)S(1)}, u32[]{:S(2)}) copy-start(bf16[6,512,128]{2,1,0:T(8,128)(2,1)S(1)} %get-tuple-element.352) | copy-start | bytes 2359300
  136.0 138.4 %reduce-scatter.8.cloned.1.call-start = ((), (), s32[]{:S(2)}) async-start(), calls=%async_computation.7 | async-start | bytes 4718592 | tf_op jit(solution)/shard_map/reduce_scatter | solution.py:129
  212.7 11.5 %copy-start.6 = (f32[512,1536]{1,0:T(8,128)}, f32[512,1536]{1,0:T(8,128)S(1)}, u32[]{:S(2)}) copy-start(f32[512,1536]{1,0:T(8,128)S(1)} %get-tuple-element.189) | copy-start | bytes 9437188
  219.7 5.7 copy-start.15
  224.2 1.1 copy-start.11
  229.7 123.8 %all-gather.11.cloned.1.call-start = ((), (), s32[]{:S(2)}) async-start(), calls=%async_computation.8 | async-start | bytes 2359296 | tf_op jit(solution)/shard_map/all_gather | solution.py:135
  325.3 0.9 copy-start.3
  326.2 27.4 %copy-start.10 = (bf16[512,1536]{1,0:T(8,128)(2,1)S(1)}, bf16[512,1536]{1,0:T(8,128)(2,1)}, u32[]{:S(2)}) copy-start(bf16[512,1536]{1,0:T(8,128)(2,1)} %param.11) | copy-start | bytes 4718596
  326.2 251.7 %reduce-scatter.10.cloned.1.call-start = ((), (), s32[]{:S(2)}) async-start(), calls=%async_computation.9 | async-start | bytes 20054016 | tf_op jit(solution)/shard_map/reduce_scatter | solution.py:139
  353.5 4.3 copy-start
  383.6 1.1 copy-start.4
  383.7 3.4 copy-start.9
  387.1 190.8 %copy-start.1 = (bf16[96,1536]{1,0:T(8,128)(2,1)S(1)}, bf16[96,1536]{1,0:T(8,128)(2,1)}, u32[]{:S(2)}) copy-start(bf16[96,1536]{1,0:T(8,128)(2,1)} %param.14) | copy-start | bytes 884740
Sparse Core Ops, SparseCore 0:
  16.3 54.9 all-gather.4
  78.6 41.9 reduce-scatter.5
  123.4 53.1 all-gather.8
  178.6 25.7 all-gather.6
  229.8 44.5 reduce-scatter.7
  326.3 27.1 all-gather.10
  383.8 194.0 reduce-scatter.9
where the time goes:
time: 595 us; the launch traced here: 594 us
  waiting for transfers between devices  407 us (68%)
  matrix products  89.7 us (15%)
  local copies, waits for them, and re-layouts  37.6 us (6%)
  other arithmetic  26.8 us (5%)
  blocking collectives  17.7 us (3%)
  between operations  14.3 us (2%)
    reduce_scatter x1, waiting for transfers between devices, shards(): lax.psum_scatter(jnp.concatenate((contract_first(grad_values, hidden), co...  181 us
    all_gather x1, waiting for transfers between devices, shards(): lax.all_gather(unit_v.astype(jnp.bfloat16), 'fsdp', axis=0, tiled=True)  55 us
    reduce_scatter x1, waiting for transfers between devices, shards(): lax.psum_scatter(grad_attn_parts, 'grp', scatter_dimension=1, tiled=True)  44.7 us
    all_gather x1, waiting for transfers between devices, shards(): lax.all_gather(unit_o.astype(jnp.bfloat16), 'fsdp', axis=0, tiled=True)  40.5 us
    reduce_scatter x1, waiting for transfers between devices, shards(): lax.psum_scatter(value_parts, 'grp', scatter_dimension=1, tiled=True)  39 us
    dot_general x20, matrix products, contract_last(): lax.dot_general(left, right, (((1,), (1,)), ((), ())), preferred_element_...  28.7 us
    all_gather x1, waiting for transfers between devices, shards(): attn_all = lax.all_gather(attn_mine, 'grp', axis=1, tiled=True)  27.7 us
    dot_general x14, matrix products, contract_first(): lax.dot_general(left, right, (((0,), (0,)), ((), ())), preferred_element_...  27.4 us
  transfers between devices with their start and end apart: 7, of which 7 were waited for; matrix products, arithmetic and copies ran while one was open for 6% of the time, Pallas kernels for 0%

commit v1 on v0

--- a/solution.py
+++ b/solution.py
@@ -6,6 +6,11 @@
 D = 3072
 HS = 128
 EPS = 1e-06
+
+
+def gather_by_exchange(array, axis, dim):
+    copies = jnp.concatenate([array] * lax.axis_size(axis), axis=dim)
+    return lax.all_to_all(copies, axis, dim, dim, tiled=True)
 
 
 def contract_last(left, right):
@@ -77,7 +82,7 @@
     unit_o = out_rows / norm_o
     weight_v, weight_o = (
         lax.all_gather(unit_v.astype(jnp.bfloat16), "fsdp", axis=0, tiled=True),
-        lax.all_gather(unit_o.astype(jnp.bfloat16), "fsdp", axis=0, tiled=True),
+        gather_by_exchange(unit_o.astype(jnp.bfloat16), "fsdp", 0),
     )
     value_parts = contract_last(hidden, weight_v)
     values_mine = lax.psum_scatter(value_parts, "grp", scatter_dimension=1, tiled=True).astype(

time: 595 us -> 585 us (0.983)
  waiting for transfers between devices: 407 us -> 373 us
  other arithmetic: 26.8 us -> 42.3 us
    all_gather x1 -> x0, waiting for transfers between devices: 40.5 us -> none  [shards(): lax.all_gather(unit_o.astype(jnp.bfloat16), 'fsdp', axis=0, tiled=True)]
    all_to_all x0 -> x1, waiting for transfers between devices: none -> 39.6 us  [gather_by_exchange(): return lax.all_to_all(copies, axis, dim, dim, tiled=True)]
    all_gather x1, waiting for transfers between devices: 27.7 us -> 0.01 us  [shards(): attn_all = lax.all_gather(attn_mine, 'grp', axis=1, tiled=True)]
    unnamed x0 -> x15, other arithmetic: none -> 15.5 us
    reduce_scatter x1, waiting for transfers between devices: 44.7 us -> 59.6 us  [shards(): lax.psum_scatter(grad_attn_parts, 'grp', scatter_dimension=1, tiled=True)]
    all_gather x1, waiting for transfers between devices: 55 us -> 44.6 us  [shards(): lax.all_gather(unit_v.astype(jnp.bfloat16), 'fsdp', axis=0, tiled=True)]
    reduce_scatter x1, waiting for transfers between devices: 39 us -> 29.7 us  [shards(): lax.psum_scatter(value_parts, 'grp', scatter_dimension=1, tiled=True)]
  transfers between devices with their start and end apart: 7 -> 7, of which waited for: 7 -> 6; matrix products, arithmetic and copies ran while one was open for 6% -> 9% of each run, Pallas kernels for 0% -> 0%
where the time goes in v1:
time: 585 us; the launch traced here: 583 us
  waiting for transfers between devices  373 us (64%)
  matrix products  91.5 us (16%)
  other arithmetic  42.3 us (7%)
  local copies, waits for them, and re-layouts  37.1 us (6%)
  blocking collectives  19.1 us (3%)
  between operations  14.4 us (2%)
    reduce_scatter x1, waiting for transfers between devices, shards(): lax.psum_scatter(jnp.concatenate((contract_first(grad_values, hidden), co...  181 us
    reduce_scatter x1, waiting for transfers between devices, shards(): lax.psum_scatter(grad_attn_parts, 'grp', scatter_dimension=1, tiled=True)  59.6 us
    all_gather x1, waiting for transfers between devices, shards(): lax.all_gather(unit_v.astype(jnp.bfloat16), 'fsdp', axis=0, tiled=True)  44.6 us
    all_to_all x1, waiting for transfers between devices, gather_by_exchange(): return lax.all_to_all(copies, axis, dim, dim, tiled=True)  39.6 us
    dot_general x20, matrix products, contract_last(): lax.dot_general(left, right, (((1,), (1,)), ((), ())), preferred_element_...  30.5 us
    reduce_scatter x1, waiting for transfers between devices, shards(): lax.psum_scatter(value_parts, 'grp', scatter_dimension=1, tiled=True)  29.7 us
    dot_general x14, matrix products, contract_first(): lax.dot_general(left, right, (((0,), (0,)), ((), ())), preferred_element_...  27.4 us
    unnamed x37, local copies, waits for them, and re-layouts  26 us
  transfers between devices with their start and end apart: 7, of which 6 were waited for; matrix products, arithmetic and copies ran while one was open for 9% of the time, Pallas kernels for 0%

profile of v1, /device:TPU:0, one launch (start us, length us, event | category | flops | bytes accessed | tf_op | source)
XLA Modules:
  0.0 583.1 jit_solution(10828909652480373924)
XLA Ops:
  8.5 6.0 %all-reduce.2 = (f32[96]{0:T(128)S(1)}, f32[96]{0:T(128)S(1)}) all-reduce(f32[96]{0:T(128)S(1)} %get-tuple-element.190, f32[96]{0:T(128)S(1)} %get-tuple-element.191), channel_id=1, replica_groups=mesh['fsdp'=16,'grp'=2] {'grp'}, use_global_device_ids=true, to_apply=%region_1.0 | all-reduce | flops 192 | bytes 1536 | tf_op jit(solution)/shard_map/psum | solution.py:76
  14.6 1.8 fusion.60
  18.2 1.8 constant_dynamic-update-slice_fusion.18
  26.9 44.6 %all-gather.4.cloned.1.call-done = bf16[1536,1536]{1,0:T(8,128)(2,1)} async-done(((bf16[96,1536]{1,0:T(8,128)(2,1)}), bf16[1536,1536]{1,0:T(8,128)(2,1)}) %all-gather.4.cloned.1.call-update) | async-done | bytes 4718608 | tf_op jit(solution)/shard_map/all_gather | solution.py:84
  71.5 6.6 %convolution_bitcast_fusion = f32[512,1536]{0,1:T(8,128)} fusion(bf16[1536,1536]{1,0:T(8,128)(2,1)} %all-gather.4.cloned.1.call-done, bf16[512,1536]{1,0:T(8,128)(2,1)S(1)} %copy-done.10), kind=kOutput, calls=%fused_computation.68 | convolution fusion | flops 2415919104 | bytes 9437184 | tf_op jit(solution)/shard_map/dot_general | solution.py:17
  84.1 4.7 all-to-all-start
  90.6 29.7 %reduce-scatter.6.cloned.1.call-done = f32[512,768]{0,1:T(8,128)} async-done(((f32[512,1536]{0,1:T(8,128)}), f32[512,768]{0,1:T(8,128)}) %reduce-scatter.6.cloned.1.call-update) | async-done | bytes 1572880 | tf_op jit(solution)/shard_map/reduce_scatter | solution.py:88
  123.1 11.8 %while.24 = (s32[]{:T(128)}, bf16[6,512,128]{1,2,0:T(8,128)(2,1)S(1)}, bf16[6,512,128]{2,1,0:T(8,128)(2,1)S(1)}, bf16[6,512,128]{2,1,0:T(8,128)(2,1)S(1)}, bf16[6,512,128]{2,1,0:T(8,128)(2,1)}, /*index=5*/s32[]{:T(128)}) while((s32[]{:T(128)}, bf16[6,512,128]{1,2,0:T(8,128)(2,1)S(1)}, bf16[6,512,128]{2,1,0:T(8,128)(2,1)S(1)}, ...), condition=%wide.region_6.7_spmd, body=%wide.region_3.6_spmd.sunk | while | flops 136641536 | bytes 4205653 | solution.py:94
  135.8 39.6 %all-to-all-done = bf16[16,96,1536]{2,1,0:T(8,128)(2,1)} async-done(((bf16[16,96,1536]{2,1,0:T(8,128)(2,1)}), bf16[16,96,1536]{2,1,0:T(8,128)(2,1)}, u32[]{:S(2)}, u32[]{:S(2)}) %all-to-all-start) | async-done | bytes 4718624 | tf_op jit(solution)/shard_map/all_to_all | solution.py:13
  175.4 8.4 %fusion.43 = (f32[512]{0:T(512)S(1)}, f32[512]{0:T(512)S(1)}, f32[512]{0:T(512)S(1)}, f32[512]{0:T(512)S(1)}, f32[512]{0:T(512)S(1)}, /*index=5*/f32[512]{0:T(512)S(1)}, f32[512,1536]{1,0:T(8,128)S(1)}) fusion(bf16[512,1536]{1,0:T(8,128)(2,1)} %param.17, f32[1536]{0:T(1024)S(1)} %copy-done.15, f32[1536]{0:T(1024)S(1)} %get-tuple-element.182, ...), kind=kOutput, calls=%fused_computation.72 | convolution fusion | flops 2430858240 | bytes 12625920 | tf_op jit(solution)/shard_map/dot_general | solution.py:96
  183.8 8.1 %all-reduce.1 = (f32[512]{0:T(512)S(1)}, f32[512]{0:T(512)S(1)}, f32[512]{0:T(512)S(1)}, f32[512]{0:T(512)S(1)}, f32[512]{0:T(512)S(1)}, /*index=5*/f32[512]{0:T(512)S(1)}) all-reduce(f32[512]{0:T(512)S(1)} %get-tuple-element.126, f32[512]{0:T(512)S(1)} %get-tuple-element.130, ...), channel_id=1, replica_groups=mesh['fsdp'=16,'grp'=2] {'grp'}, use_global_device_ids=true, to_apply=%region_16.17 | all-reduce | flops 3072 | bytes 24576 | tf_op jit(solution)/shard_map/psum | solution.py:99
  192.0 4.4 multiply_convert_fusion.1
  197.5 6.6 %fusion.65 = f32[512,1536]{1,0:T(8,128)} fusion(bf16[512,1536]{1,0:T(8,128)(2,1)S(1)} %get-tuple-element.177, bf16[1536,1536]{1,0:T(8,128)(2,1)} %bitcast.21), kind=kOutput, calls=%fused_computation.128 | convolution fusion | flops 2415919104 | bytes 9437184 | tf_op jit(solution)/shard_map/dot_general | solution.py:17
  204.2 59.6 %reduce-scatter.8.cloned.1.call-done = f32[512,768]{1,0:T(8,128)} async-done(((f32[512,1536]{1,0:T(8,128)}), f32[512,768]{1,0:T(8,128)}) %reduce-scatter.8.cloned.1.call-update) | async-done | bytes 1572880 | tf_op jit(solution)/shard_map/reduce_scatter | solution.py:134
  267.5 47.0 %while.25 = (s32[]{:T(128)}, bf16[6,512,128]{1,2,0:T(8,128)(2,1)}, bf16[6,512,128]{1,2,0:T(8,128)(2,1)S(1)}, bf16[6,512,128]{1,2,0:T(8,128)(2,1)S(1)}, bf16[6,51...) while((s32[]{:T(128)}, bf16[6,512,128]{1,2,0:T(8,128)(2,1)}, ...), condition=%wide.region_26.27_spmd, body=%wide.region_22.26_spmd.sunk | while | flops 340589056 | bytes 11821177 | solution.py:137
  315.5 8.5 %fusion.67 = f32[1536,1536]{0,1:T(8,128)} fusion(bf16[512,1536]{0,1:T(8,128)(2,1)} %all-gather.6.cloned.1.call-done, bf16[512,1536]{1,0:T(8,128)(2,1)} %copy-done.12), kind=kOutput, calls=%fused_computation.130 | convolution fusion | flops 2415919104 | bytes 12582912 | tf_op jit(solution)/shard_map/dot_general | solution.py:23
  324.0 18.8 %all-gather.8.cloned.1.call-done = bf16[512,1536]{0,1:T(8,128)(2,1)} async-done(((bf16[512,768]{0,1:T(8,128)(2,1)}), bf16[512,1536]{0,1:T(8,128)(2,1)}) %all-gather.8.cloned.1.call-update) | async-done | bytes 1572880 | tf_op jit(solution)/shard_map/all_gather | solution.py:140
  342.8 4.2 fusion.66
  347.1 7.2 %pad_maximum_fusion = f32[1536,3072]{0,1:T(8,128)} fusion(f32[1536,1536]{0,1:T(8,128)S(1)} %copy-done.1, f32[1536,1536]{0,1:T(8,128)S(1)} %fusion.66), kind=kLoop, calls=%fused_computation.57 | loop fusion | flops 4718592 | bytes 37748736 | tf_op jit(solution)/shard_map/concatenate | solution.py:145
  354.3 18.7 %copy.58 = f32[1536,3072]{1,0:T(8,128)} copy(f32[1536,3072]{0,1:T(8,128)} %pad_maximum_fusion) | data formatting | bytes 37748736
  376.4 10.0 %fusion.51 = bf16[512,1536]{1,0:T(8,128)(2,1)} fusion(bf16[512,1536]{0,1:T(8,128)(2,1)} %all-gather.8.cloned.1.call-done, bf16[1536,1536]{1,0:T(8,128)(2,1)} %all-gather.4.cloned.1.call-done, bf16[512,1536]{1,0:T(8,128)(2,1)S(1)} %copy-done.9, f32[512]{0:T(512)S(1)} %get-tuple-element.187, f32[1536]{0:T(1024)S(1)} %get-tuple-element.185, ...), kind=kOutput, calls=%fused_computation.82 | convolution fusion | flops 2426929152 | bytes 14174208 | tf_op jit(solution)/shard_map/dot_general | solution.py:142
  386.4 180.8 %reduce-scatter.10.cloned.1.call-done = f32[96,3072]{1,0:T(8,128)} async-done(((f32[1536,3072]{1,0:T(8,128)}), f32[96,3072]{1,0:T(8,128)}) %reduce-scatter.10.cloned.1.call-update) | async-done | bytes 1179664 | tf_op jit(solution)/shard_map/reduce_scatter | solution.py:144
  568.8 4.9 all-reduce
  573.7 2.5 subtract_divide_fusion
  (182 shorter events, 90.6 us)
Async XLA Ops:
  7.2 14.7 %copy-start = (bf16[96,1536]{1,0:T(8,128)(2,1)S(1)}, bf16[96,1536]{1,0:T(8,128)(2,1)}, u32[]{:S(2)}) copy-start(bf16[96,1536]{1,0:T(8,128)(2,1)} %param.15) | copy-start | bytes 884740
  7.2 64.3 %all-gather.4.cloned.1.call-start = ((), (), s32[]{:S(2)}) async-start(), calls=%async_computation.4 | async-start | bytes 5013504 | tf_op jit(solution)/shard_map/all_gather | solution.py:84
  8.5 63.0 %copy-start.10 = (bf16[512,1536]{1,0:T(8,128)(2,1)S(1)}, bf16[512,1536]{1,0:T(8,128)(2,1)}, u32[]{:S(2)}) copy-start(bf16[512,1536]{1,0:T(8,128)(2,1)} %param.11) | copy-start | bytes 4718596
  16.4 103.9 %reduce-scatter.6.cloned.1.call-start = ((), (), s32[]{:S(2)}) async-start(), calls=%async_computation.5 | async-start | bytes 4718592 | tf_op jit(solution)/shard_map/reduce_scatter | solution.py:88
  84.1 4.8 copy-start.13
  84.1 91.3 %all-to-all-start = ((bf16[16,96,1536]{2,1,0:T(8,128)(2,1)}), bf16[16,96,1536]{2,1,0:T(8,128)(2,1)}, u32[]{:S(2)}, u32[]{:S(2)}) async-start(bf16[16,96,1536]{2,1,0:T(8,128)(2,1)} %bitcast.20), calls=%async_computation.1 | async-start | bytes 9437184 | tf_op jit(solution)/shard_map/all_to_all | solution.py:13
  88.8 1.1 copy-start.14
  88.8 86.6 %all-gather.6.cloned.1.call-start = ((), (), s32[]{:S(2)}) async-start(), calls=%async_computation.6 | async-start | bytes 2359296 | tf_op jit(solution)/shard_map/all_gather | solution.py:95
  123.0 12.7 %copy-start.15 = (f32[1536]{0:T(1024)S(1)}, f32[1536]{0:T(1024)}, u32[]{:S(2)}) copy-start(f32[1536]{0:T(1024)} %param.16) | copy-start | bytes 18436
  134.8 0.9 copy-start.5
  134.8 40.6 %copy-start.7 = (bf16[6,512,128]{2,1,0:T(8,128)(2,1)}, bf16[6,512,128]{2,1,0:T(8,128)(2,1)S(1)}, u32[]{:S(2)}) copy-start(bf16[6,512,128]{2,1,0:T(8,128)(2,1)S(1)} %get-tuple-element.350) | copy-start | bytes 2359300
  134.8 40.6 %copy-start.8 = (bf16[6,512,128]{2,1,0:T(8,128)(2,1)}, bf16[6,512,128]{2,1,0:T(8,128)(2,1)S(1)}, u32[]{:S(2)}) copy-start(bf16[6,512,128]{2,1,0:T(8,128)(2,1)S(1)} %get-tuple-element.351) | copy-start | bytes 2359300
  135.7 128.1 %reduce-scatter.8.cloned.1.call-start = ((), (), s32[]{:S(2)}) async-start(), calls=%async_computation.7 | async-start | bytes 4718592 | tf_op jit(solution)/shard_map/reduce_scatter | solution.py:134
  183.8 12.5 %copy-start.6 = (f32[512,1536]{1,0:T(8,128)}, f32[512,1536]{1,0:T(8,128)S(1)}, u32[]{:S(2)}) copy-start(f32[512,1536]{1,0:T(8,128)S(1)} %get-tuple-element.189) | copy-start | bytes 9437188
  196.4 1.1 copy-start.12
  204.2 138.7 %all-gather.8.cloned.1.call-start = ((), (), s32[]{:S(2)}) async-start(), calls=%async_computation.8 | async-start | bytes 2359296 | tf_op jit(solution)/shard_map/all_gather | solution.py:140
  314.6 0.9 copy-start.3
  315.5 27.4 %copy-start.11 = (bf16[512,1536]{1,0:T(8,128)(2,1)S(1)}, bf16[512,1536]{1,0:T(8,128)(2,1)}, u32[]{:S(2)}) copy-start(bf16[512,1536]{1,0:T(8,128)(2,1)} %param.11) | copy-start | bytes 4718596
  315.5 251.7 %reduce-scatter.10.cloned.1.call-start = ((), (), s32[]{:S(2)}) async-start(), calls=%async_computation.9 | async-start | bytes 20054016 | tf_op jit(solution)/shard_map/reduce_scatter | solution.py:144
  342.8 4.3 copy-start.1
  372.9 1.1 copy-start.4
  373.0 3.4 copy-start.9
  376.4 190.8 %copy-start.2 = (bf16[96,1536]{1,0:T(8,128)(2,1)S(1)}, bf16[96,1536]{1,0:T(8,128)(2,1)}, u32[]{:S(2)}) copy-start(bf16[96,1536]{1,0:T(8,128)(2,1)} %param.14) | copy-start | bytes 884740
Sparse Core Ops, SparseCore 0:
  16.5 54.9 all-gather.3
  78.2 42.0 reduce-scatter.5
  135.8 27.1 all-gather.5
  204.3 59.4 reduce-scatter.7
  315.6 27.1 all-gather.7
  373.1 194.0 reduce-scatter.9
